TPU v7x, 32 devices: a whole 2x2x4 slice. The times are simulated.
32 devices in a mesh: img: 2 (over x), neu: 16 (over z, y, core).
Axes of the slice: x: 2, y: 2, z: 4, core: 2. Of those that a mesh axis runs over, the one named last changes fastest.
Arguments:
- image_values: bfloat16 [4096, 1024], P('neu', 'img'), may hold values from 0.25 to 16
- image_mask: int32 [4096, 1024], P('neu', 'img'), may hold values 0 or 1
- weights: bfloat16 [3, 4096, 4, 8], P(None, 'neu'), may hold values from -0.25 to 0.34960938
- block_index: int32 [3, 128, 4], P(None, 'neu'), may hold values from 0 to 511, as said below
Outputs:
- activations: bfloat16 [4096, 1024], P('neu', 'img')
- row_sums: float32 [1024], P(('img', 'neu'))
Inputs may be any that keep to these rules, and one draw needn't show every extreme that they name: Split the 512 input blocks into 16 runs of consecutive blocks, and the 128 output blocks likewise; if output block b lies in run s, block_index[l, b, k] lies in run (s + k * 4 + l) mod 16.
All inputs are finite; a program needn't handle non-finite values. No bound on the sum of `image_mask` on one device may be relied on, other than what follows from the above.
Results may differ from a plain program's by a relative error of at most 0.0035.
Values may be sent and summed in bfloat16 or wider, within the bound.
A program may use at most 64 MiB of HBM per device.

v0:
```python
import functools

import jax
import jax.numpy as jnp
from jax import lax
from jax.experimental import pallas as pl
from jax.experimental.pallas import tpu as pltpu
from jax.sharding import PartitionSpec as P

KB = 4
IB = 8
OB = 32

bias_value = 0.35
ceiling = 32.0


def quotient(x, n):
    return x >> (n.bit_length() - 1) if n & (n - 1) == 0 else lax.div(x, jnp.int32(n))


def remainder(x, n):
    return x & (n - 1) if n & (n - 1) == 0 else lax.rem(x, jnp.int32(n))


def kernel(
    geometry, val_hbm, mask_hbm, wt_hbm, idx_hbm, out_ref, rs_ref,
    val, mask, w_src, i_src, y0, xin, ya, yb, wt, wd, idx_v, idx_s, tiles, part, parts,
    load_sem, own_sem, f_send, f_recv, in_send, in_recv, w_send, w_recv, i_send, i_recv, s_sem, o_send, o_recv, r_send, r_recv,
):
    classes, pairs, layers, rows, blocks, lanes = geometry
    group = KB
    devices = classes * group
    shift = [l * (l + 1) // 2 for l in range(layers)]
    me = lax.axis_index("neu")
    q, c = me // classes, me % classes
    run_blocks = rows // IB

    def device(dq, dc):
        return ((q + dq) % group) * classes + (c + dc) % classes

    def remote(src, dst, send, recv, dq, dc):
        return pltpu.make_async_remote_copy(
            src_ref=src, dst_ref=dst, send_sem=send, recv_sem=recv,
            device_id={"neu": device(dq, dc)}, device_id_type=pl.DeviceIdType.MESH,
        )

    order = [1, 3, 2]
    order_w = [1, 3, 2]
    order_in = [1, 2, 3]
    order_out = [1, 3, 2]

    own = [
        pltpu.make_async_copy(wt_hbm, w_src, own_sem.at[0]),
        pltpu.make_async_copy(idx_hbm, i_src, own_sem.at[1]),
    ]
    loads = []
    for d in order + [0]:
        t = (q + d) % group
        cols = pl.ds(pl.multiple_of(t * lanes, lanes), lanes)
        a = pltpu.make_async_copy(val_hbm.at[:, cols], val.at[d], load_sem.at[0, d])
        b = pltpu.make_async_copy(mask_hbm.at[:, cols], mask.at[d], load_sem.at[1, d])
        loads.append((d, a, b))
    for a in own:
        a.start()
    for d, a, b in loads:
        a.start()
        b.start()

    partners = set()
    for dq in range(group):
        for s in shift:
            partners |= {(dq, s % classes), (dq, -s % classes)}
    for dc in range(classes):
        partners.add((0, dc))
    partners.discard((0, 0))
    barrier = pltpu.get_barrier_semaphore()
    for dq, dc in sorted(partners, reverse=True):
        pl.semaphore_signal(
            barrier, inc=1, device_id={"neu": device(dq, dc)},
            device_id_type=pl.DeviceIdType.MESH,
        )
    if pairs:
        x_me = lax.axis_index("img")
        half = x_me % 2
        twin = x_me + 1 - 2 * half
        share_rows = KB * IB // 2
        w_rows = pl.ds(pl.multiple_of(half * share_rows, share_rows), share_rows)
        pl.semaphore_signal(
            barrier, inc=1, device_id={"img": twin}, device_id_type=pl.DeviceIdType.MESH
        )
    else:
        w_rows = pl.ds(0, KB * IB)

    for d, a, b in loads:
        a.wait()
        b.wait()
        masked = (val[d].astype(jnp.float32) * mask[d].astype(jnp.float32))
        if d:
            y0[d] = masked.astype(jnp.bfloat16)
        else:
            ya[pl.ds(q * run_blocks, run_blocks)] = masked.reshape(run_blocks, IB, lanes)
    for a in own:
        a.wait()
    pl.semaphore_wait(barrier, len(partners) + (1 if pairs else 0))

    waits = []
    index_waits = [[] for _ in range(layers)]
    weight_sends = []
    weight_waits = [[] for _ in range(layers)]
    for l in range(layers):
        for dq in order_w + [0]:
            if dq == 0 and shift[l] % classes == 0:
                a = pltpu.make_async_copy(w_src.at[l], wt.at[l, q], w_recv.at[l, 0])
                b = pltpu.make_async_copy(i_src.at[l], idx_v.at[l, q], i_recv.at[l, 0])
                a.start()
                b.start()
                weight_waits[l].append(a.wait)
                index_waits[l].append(b.wait)
                continue
            b = remote(i_src.at[l], idx_v.at[l, q], i_send.at[l, dq], i_recv.at[l, dq], dq, shift[l])
            a = remote(
                w_src.at[l, w_rows], wt.at[l, q, w_rows], w_send.at[l, dq], w_recv.at[l, dq], dq, shift[l]
            )
            b.start()
            a.start()
            waits.extend([a.wait_send, b.wait_send])
            index_waits[l].append(b.wait_recv)
            weight_sends.append((l, dq, a))

    inputs = []
    for d in order_in:
        x = remote(y0.at[d], xin.at[d], in_send.at[d], in_recv.at[d], d, 0)
        x.start()
        waits.append(x.wait_send)
        inputs.append((d, x))

    for l, dq, a in weight_sends:
        a.wait_recv()
        if pairs:
            here = wt.at[l, (q + group - dq) % group, w_rows]
            x = pltpu.make_async_remote_copy(
                src_ref=here, dst_ref=here, send_sem=f_send.at[l, dq], recv_sem=f_recv.at[l, dq],
                device_id={"img": twin}, device_id_type=pl.DeviceIdType.MESH,
            )
            x.start()
            waits.append(x.wait_send)
            weight_waits[l].append(x.wait_recv)

    index_copies = []
    for l in range(layers):
        for w in index_waits[l]:
            w()
        x = pltpu.make_async_copy(idx_v.at[l], idx_s.at[l], s_sem.at[l])
        x.start()
        index_copies.append(x)

    per = min(4, blocks)
    width = per * OB
    m_of = lax.broadcasted_iota(jnp.int32, (width, width), 0) // (KB * IB)
    n_of = lax.broadcasted_iota(jnp.int32, (width, width), 1) // OB

    def prepare(l):
        for w in weight_waits[l]:
            w()
        for t in range(group):
            for g in range(blocks // per):
                w = wt[l, t, :, g * width:(g + 1) * width].astype(jnp.float32)
                wide = jnp.where(m_of == n_of, jnp.concatenate([w] * per, axis=0), 0.0)
                wd[l, t, g] = wide.T.astype(jnp.bfloat16)

    def advance(l, src, t):
        out = []
        for g in range(blocks // per):
            pieces = []
            for j in range(g * per, (g + 1) * per):
                for k in range(KB):
                    b = idx_s[l, t, k, j]
                    pieces.append(src[quotient(b, run_blocks * classes) * run_blocks + remainder(b, run_blocks)])
            picked = jnp.concatenate(pieces, axis=0).astype(jnp.bfloat16)
            summed = jnp.dot(wd[l, t, g], picked, preferred_element_type=jnp.float32)
            clamped = jnp.minimum(jnp.maximum(summed - bias_value, 0.0), ceiling)
            out.append(clamped.astype(jnp.bfloat16))
        return out

    for l in range(layers):
        prepare(l)
    for x in index_copies:
        x.wait()
    for d, x in inputs:
        x.wait_recv()
        s = (q + group - d) % group
        ya[pl.ds(s * run_blocks, run_blocks)] = xin[d].astype(jnp.float32).reshape(run_blocks, IB, lanes)

    src, dst = ya, yb
    for l in range(layers - 1):
        for t in range(group):
            for g, y in enumerate(advance(l, src, t)):
                first = t * run_blocks + g * width // IB
                dst[first:first + width // IB] = y.astype(jnp.float32).reshape(width // IB, IB, lanes)
        src, dst = dst, src

    total = jnp.zeros((8, lanes), jnp.float32)
    last = layers - 1
    outputs = []
    for d in order_out + [0]:
        t = (q + d) % group
        for g, y in enumerate(advance(last, src, t)):
            tiles[d, g * width:(g + 1) * width, :] = y
            total = total + jnp.sum(y.astype(jnp.float32).reshape(width // 8, 8, lanes), axis=0)
        x = remote(
            tiles.at[d], out_ref.at[:, pl.ds(pl.multiple_of(q * lanes, lanes), lanes)],
            o_send.at[d], o_recv.at[d], d, -shift[last],
        )
        x.start()
        waits.append(x.wait_send)
        outputs.append(x)

    part[...] = total
    sums = []
    for dc in range(1, classes):
        x = remote(part, parts.at[dc], r_send.at[dc], r_recv.at[dc], 0, dc)
        x.start()
        waits.append(x.wait_send)
        sums.append((dc, x))
    for dc, x in sums:
        x.wait_recv()
        total = total + parts[dc]
    row = jnp.sum(total, axis=0, keepdims=True)
    share = lanes // classes
    mine = jnp.zeros((1, share), jnp.float32)
    for j in range(classes):
        mine = jnp.where(c == j, row[:, j * share:(j + 1) * share], mine)
    rs_ref[...] = mine
    for x in outputs:
        x.wait_recv()
    for w in waits:
        w()


def on_device(classes, pairs, image_values, image_mask, weights, block_index):
    layers, rows = weights.shape[:2]
    blocks = block_index.shape[1]
    columns = image_values.shape[1]
    group = KB
    lanes = columns // group
    wt = jnp.transpose(weights, (0, 2, 3, 1)).reshape(layers, KB * IB, rows)
    idx = jnp.transpose(block_index, (0, 2, 1))
    per = min(4, blocks)
    bf16, f32, i32 = jnp.bfloat16, jnp.float32, jnp.int32
    V, S = pltpu.VMEM, pltpu.SMEM
    dma = pltpu.SemaphoreType.DMA
    any_spec = pl.BlockSpec(memory_space=pl.ANY)
    operands = [pltpu.with_memory_space_constraint(v, pltpu.HBM) for v in (image_values, image_mask, wt, idx)]
    out, sums = pl.pallas_call(
        functools.partial(kernel, (classes, pairs, layers, rows, blocks, lanes)),
        out_shape=(
            jax.ShapeDtypeStruct((rows, columns), bf16),
            jax.ShapeDtypeStruct((1, lanes // classes), f32),
        ),
        in_specs=[any_spec] * 4,
        out_specs=(pl.BlockSpec(memory_space=pltpu.VMEM), pl.BlockSpec(memory_space=pltpu.VMEM)),
        scratch_shapes=[
            V((group, rows, lanes), bf16),
            V((group, rows, lanes), i32),
            V((layers, KB * IB, rows), bf16),
            V((layers, KB, blocks), i32),
            V((group, rows, lanes), bf16),
            V((group, rows, lanes), bf16),
            V((group * rows // IB, IB, lanes), f32),
            V((group * rows // IB, IB, lanes), f32),
            V((layers, group, KB * IB, rows), bf16),
            V((layers, group, blocks // per, per * OB, per * KB * IB), bf16),
            V((layers, group, KB, blocks), i32),
            S((layers, group, KB, blocks), i32),
            V((group, rows, lanes), bf16),
            V((8, lanes), f32),
            V((classes, 8, lanes), f32),
            dma((2, group)), dma((2,)),
            dma((layers, group)), dma((layers, group)),
            dma((group,)), dma((group,)),
            dma((layers, group)), dma((layers, group)),
            dma((layers, group)), dma((layers, group)),
            dma((layers,)),
            dma((group,)), dma((group,)),
            dma((classes,)), dma((classes,)),
        ],
        compiler_params=pltpu.CompilerParams(collective_id=0, has_side_effects=True, vmem_limit_bytes=16 * 1024 * 1024),
    )(*operands)
    return out, sums.reshape(-1)


def solution(mesh):
    classes = mesh.shape["neu"] // KB
    in_specs = (P("neu", "img"), P("neu", "img"), P(None, "neu", None, None), P(None, "neu", None))
    out_specs = (P("neu", "img"), P(("img", "neu")))
    return jax.shard_map(
        functools.partial(on_device, classes, mesh.shape["img"] % 2 == 0), mesh=mesh, in_specs=in_specs,
        out_specs=out_specs, check_vma=False,
    )
```

profile of v0, /device:TPU:0, one launch (start us, length us, event | category | flops | bytes accessed | tf_op | source)
XLA Modules:
  0.0 24.6 jit_solution(14544074356083312127)
XLA Ops:
  0.6 22.8 %shard_map.59 = (bf16[256,512]{1,0:T(8,128)(2,1)S(1)}, f32[1,32]{1,0:T(1,128)S(1)}) custom-call(bf16[256,512]{1,0:T(8,128)(2,1)} %val_hbm.1, s32[256,512]{1,0:T(8,128)} %mask_hbm.1, bf16[3,32,256]{2,1,0:T(8,128)(2,1)} %bitcast.6, s32[3,4,8]{2,1,0:T(4,128)} %bitcast.7), custom_call_target="tpu_custom_call" | custom-call | tf_op jit(solution)/shard_map/pallas_call | solution.py:255
  23.4 0.7 %copy.8 = bf16[256,512]{1,0:T(8,128)(2,1)} copy(bf16[256,512]{1,0:T(8,128)(2,1)S(1)} %get-tuple-element.8) | data formatting | bytes 524288
  24.1 0.5 %copy.9 = f32[32]{0:T(128)} copy(f32[32]{0:T(128)S(1)} %bitcast.5) | data formatting | bytes 256
where the time goes:
time: 24.9 us; the launch traced here: 24.6 us
  Pallas kernels  22.8 us (92%)
  local copies, waits for them, and re-layouts  1.22 us (5%)
  between operations  0.64 us (3%)
    pallas_call x1, Pallas kernels, on_device(): pl.pallas_call(functools.partial(kernel, (classes, pairs, layers, rows, b...  22.8 us
    unnamed x2, local copies, waits for them, and re-layouts  1.22 us

commit v1 on v0

v1 whole, which is shorter than its diff:
```python
import functools

import jax
import jax.numpy as jnp
from jax import lax
from jax.experimental import pallas as pl
from jax.experimental.pallas import tpu as pltpu
from jax.sharding import PartitionSpec as P

KB = 4
IB = 8
OB = 32

bias_value = 0.35
ceiling = 32.0


def quotient(x, n):
    return x >> (n.bit_length() - 1) if n & (n - 1) == 0 else lax.div(x, jnp.int32(n))


def remainder(x, n):
    return x & (n - 1) if n & (n - 1) == 0 else lax.rem(x, jnp.int32(n))


def by_position(q, values):
    return (sum(v << (2 * i) for i, v in enumerate(values)) >> (2 * q)) & 3


def kernel(
    geometry, val_hbm, mask_hbm, wt_hbm, idx_hbm, out_ref, rs_ref,
    val, mask, w_src, i_src, i_out, y0, xin, ya, yb, wt, wd, idx_v, idx_s, tiles, part, parts,
    load_sem, own_sem, w_send, w_recv, f_recv, i_send, i_recv, s_sem, in_send, in_recv, o_send, o_recv,
    r_send, r_recv, here_sem,
):
    classes, pairs, layers, rows, blocks, lanes = geometry
    group = KB
    last = layers - 1
    shift = [l * (l + 1) // 2 % classes for l in range(layers)]
    me = lax.axis_index("neu")
    q, c = me // classes, me % classes
    run_blocks = rows // IB

    middle = (q == 1) | (q == 2)
    other = by_position(q, [3, 2, 1, 0])
    near = by_position(q, [1, 0, 3, 2])
    far = by_position(q, [2, 3, 0, 1])
    order = [
        by_position(q, [3, 3, 0, 0]), by_position(q, [0, 2, 1, 3]),
        by_position(q, [2, 0, 3, 1]), by_position(q, [1, 1, 2, 2]),
    ]

    def to(z, dc):
        return {"neu": z * classes + (c + dc) % classes}

    def remote(src, dst, send, recv, device_id):
        x = pltpu.make_async_remote_copy(
            src_ref=src, dst_ref=dst, send_sem=send, recv_sem=recv,
            device_id=device_id, device_id_type=pl.DeviceIdType.MESH,
        )
        x.start()

    def wait(ref, sem):
        pltpu.make_async_copy(ref, ref, sem).wait()

    own = [
        pltpu.make_async_copy(wt_hbm, w_src, own_sem.at[0]),
        pltpu.make_async_copy(idx_hbm, i_src, own_sem.at[1]),
    ]
    for a in own:
        a.start()
    for p, t in enumerate(order):
        cols = pl.ds(pl.multiple_of(t * lanes, lanes), lanes)
        pltpu.make_async_copy(val_hbm.at[:, cols], val.at[p], load_sem.at[0]).start()
        pltpu.make_async_copy(mask_hbm.at[:, cols], mask.at[p], load_sem.at[1]).start()

    barrier = pltpu.get_barrier_semaphore()
    x_me = lax.axis_index("img")
    half = x_me % 2
    twin = {"img": x_me + 1 - 2 * half}
    share_rows = KB * IB // 2
    w_rows = pl.ds(pl.multiple_of(half * share_rows, share_rows), share_rows) if pairs else pl.ds(0, KB * IB)

    @pl.when(middle)
    def _():
        greet = [to(z, -s) for s in sorted(set(shift)) for z in (far, other)]
        greet += [to(near, dc) for dc in range(classes)]
        greet += [to(q, dc) for dc in range(1, classes)]
        if pairs:
            greet.append(twin)
        for device in greet:
            pl.semaphore_signal(barrier, inc=1, device_id=device, device_id_type=pl.DeviceIdType.MESH)

    def masked(p):
        y0[p] = (val[p].astype(jnp.float32) * mask[p].astype(jnp.float32)).astype(jnp.bfloat16)

    for a in own:
        a.wait()
    b = i_src[...]
    i_out[...] = quotient(b, run_blocks * classes) * run_blocks + remainder(b, run_blocks)

    def send_weights(l, z):
        n = q * layers + l
        remote(i_out.at[l], idx_v.at[n], i_send, i_recv, to(z, shift[l]))
        remote(w_src.at[l, w_rows], wt.at[n, w_rows], w_send, w_recv.at[q], to(z, shift[l]))

    def send_input(p, chunk, z):
        remote(y0.at[p], xin.at[chunk, q], in_send, in_recv.at[chunk], to(z, 0))

    unknown = [dc for dc in range(classes) if dc not in shift]

    def own_share(total):
        row = jnp.sum(total, axis=0, keepdims=True)
        share = lanes // classes
        mine = jnp.zeros((1, share), jnp.float32)
        for j in range(classes):
            mine = jnp.where(c == j, row[:, j * share:(j + 1) * share], mine)
        rs_ref[...] = mine

    @pl.when(jnp.logical_not(middle))
    def _():
        pl.semaphore_wait(barrier, classes + len(set(shift)))
        for z in (far, near):
            for l in range(layers):
                send_weights(l, z)
        for dc in unknown:
            pl.semaphore_signal(here_sem, inc=1, device_id=to(near, dc), device_id_type=pl.DeviceIdType.MESH)
        wait(val, load_sem.at[0])
        wait(mask, load_sem.at[1])
        for p in range(group):
            masked(p)
            send_input(p, p // 2, (far, near)[p % 2])
        sent = wt.at[pl.ds(0, 2 * layers), w_rows]
        wait(sent, w_send)
        wait(idx_v.at[pl.ds(0, 2 * layers)], i_send)
        wait(y0, in_send)
        wait(parts.at[pl.ds(0, classes)], r_recv.at[0])
        own_share(sum(parts[dc] for dc in range(classes)))
        wait(out_ref, o_recv)

    @pl.when(middle)
    def _():
        pl.semaphore_wait(barrier, classes - 1 + len(set(shift)) + (1 if pairs else 0))
        for l in range(layers):
            send_weights(l, other)
        for l in range(layers):
            if shift[l]:
                send_weights(l, q)
            else:
                wt[q * layers + l] = w_src[l]
                idx_v[q * layers + l] = i_out[l]
        wait(val, load_sem.at[0])
        wait(mask, load_sem.at[1])
        masked(0)
        send_input(0, 0, other)
        masked(1)
        send_input(1, 1, other)
        masked(2)
        masked(3)

        local = sum(1 for s in shift if s == 0)
        per = min(4, blocks)
        width = per * OB
        m_of = lax.broadcasted_iota(jnp.int32, (width, width), 0) // (KB * IB)
        n_of = lax.broadcasted_iota(jnp.int32, (width, width), 1) // OB

        def pieces_of(z):
            first = local if z is q else 0
            return wt.at[pl.ds(z * layers + first, layers - first), w_rows]

        def pass_on(z):
            here = pieces_of(z)
            wait(here, w_recv.at[z])
            if pairs:
                remote(here, here, w_send, f_recv.at[z], twin)

        def prepare(z):
            if pairs:
                wait(pieces_of(z), f_recv.at[z])
            for l in range(layers):
                for g in range(blocks // per):
                    w = wt[z * layers + l, :, g * width:(g + 1) * width].astype(jnp.float32)
                    wide = jnp.where(m_of == n_of, jnp.concatenate([w] * per, axis=0), 0.0)
                    wd[l, z, g] = wide.T.astype(jnp.bfloat16)

        def advance(l, src, t):
            out = []
            for g in range(blocks // per):
                pieces = [src[idx_s[t * layers + l, k, j]] for j in range(g * per, (g + 1) * per) for k in range(KB)]
                picked = jnp.concatenate(pieces, axis=0).astype(jnp.bfloat16)
                summed = jnp.dot(wd[l, t, g], picked, preferred_element_type=jnp.float32)
                clamped = jnp.minimum(jnp.maximum(summed - bias_value, 0.0), ceiling)
                out.append(clamped.astype(jnp.bfloat16))
            return out

        for z in (q, other, near, far):
            pass_on(z)
        wait(idx_v.at[pl.ds(0, group * layers - local)], i_recv)
        index_copy = pltpu.make_async_copy(idx_v, idx_s, s_sem)
        index_copy.start()
        prepare(q)
        prepare(other)
        prepare(near)
        prepare(far)
        index_copy.wait()
        pl.semaphore_wait(here_sem, len(unknown))

        for chunk in range(2):
            own_rows = y0[2 + chunk].astype(jnp.float32)
            ya[pl.ds(q * run_blocks, run_blocks)] = own_rows.reshape(run_blocks, IB, lanes)
            wait(xin.at[chunk, pl.ds(0, group - 1)], in_recv.at[chunk])
            for z in (other, near, far):
                ya[pl.ds(z * run_blocks, run_blocks)] = xin[chunk, z].astype(jnp.float32).reshape(run_blocks, IB, lanes)

            src, dst = ya, yb
            for l in range(last):
                for t in range(group):
                    for g, y in enumerate(advance(l, src, t)):
                        first = t * run_blocks + g * width // IB
                        dst[first:first + width // IB] = y.astype(jnp.float32).reshape(width // IB, IB, lanes)
                src, dst = dst, src

            tile = near if chunk == 0 else q
            cols = pl.ds(pl.multiple_of(tile * lanes, lanes), lanes)
            targets = (far, near, other, q)
            total = jnp.zeros((8, lanes), jnp.float32)

            def send_tile(d):
                remote(tiles.at[chunk, d], out_ref.at[:, cols], o_send, o_recv, to(targets[d], -shift[last]))

            ready = None
            for d in range(group + 1):
                fresh = advance(last, src, targets[d]) if d < group else None
                if ready is not None:
                    for g, y in enumerate(ready):
                        tiles[chunk, d - 1, g * width:(g + 1) * width, :] = y
                        total = total + jnp.sum(y.astype(jnp.float32).reshape(width // 8, 8, lanes), axis=0)
                    if chunk == 0:
                        send_tile(d - 1)
                ready = fresh
            part[chunk] = total
            for dc in range(chunk, classes):
                where = to(q, dc) if chunk else to(near, dc)
                remote(part.at[chunk], parts.at[chunk * classes + dc], r_send, r_recv.at[chunk], where)
            if chunk:
                for d in range(group):
                    send_tile(d)

        wait(parts.at[pl.ds(classes + 1, classes - 1)], r_recv.at[1])
        own_share(part[1] + sum(parts[classes + dc] for dc in range(1, classes)))
        if pairs:
            wait(wt.at[pl.ds(0, 3 * layers - local)], w_send)
        else:
            wait(wt.at[pl.ds(0, 2 * layers - local)], w_send)
        wait(idx_v.at[pl.ds(0, 2 * layers - local)], i_send)
        wait(y0.at[pl.ds(0, 2)], in_send)
        wait(tiles, o_send)
        wait(parts.at[pl.ds(0, 2 * classes - 1)], r_send)
        wait(out_ref, o_recv)


def store(out_ref, rs_ref, out_hbm, rs_hbm, sems):
    a = pltpu.make_async_copy(out_ref, out_hbm, sems.at[0])
    b = pltpu.make_async_copy(rs_ref, rs_hbm, sems.at[1])
    a.start()
    b.start()
    a.wait()
    b.wait()


def on_device(classes, pairs, image_values, image_mask, weights, block_index):
    layers, rows = weights.shape[:2]
    blocks = block_index.shape[1]
    columns = image_values.shape[1]
    group = KB
    lanes = columns // group
    wt = jnp.transpose(weights, (0, 2, 3, 1)).reshape(layers, KB * IB, rows)
    idx = jnp.transpose(block_index, (0, 2, 1))
    per = min(4, blocks)
    bf16, f32, i32 = jnp.bfloat16, jnp.float32, jnp.int32
    V, S = pltpu.VMEM, pltpu.SMEM
    dma = pltpu.SemaphoreType.DMA
    any_spec = pl.BlockSpec(memory_space=pl.ANY)
    operands = [pltpu.with_memory_space_constraint(v, pltpu.HBM) for v in (image_values, image_mask, wt, idx)]
    out, sums = pl.pallas_call(
        functools.partial(kernel, (classes, pairs, layers, rows, blocks, lanes)),
        out_shape=(
            jax.ShapeDtypeStruct((rows, columns), bf16),
            jax.ShapeDtypeStruct((1, lanes // classes), f32),
        ),
        in_specs=[any_spec] * 4,
        out_specs=(pl.BlockSpec(memory_space=pltpu.VMEM), pl.BlockSpec(memory_space=pltpu.VMEM)),
        scratch_shapes=[
            V((group, rows, lanes), bf16),
            V((group, rows, lanes), i32),
            V((layers, KB * IB, rows), bf16),
            V((layers, KB, blocks), i32),
            V((layers, KB, blocks), i32),
            V((group, rows, lanes), bf16),
            V((2, group, rows, lanes), bf16),
            V((group * rows // IB, IB, lanes), f32),
            V((group * rows // IB, IB, lanes), f32),
            V((group * layers, KB * IB, rows), bf16),
            V((layers, group, blocks // per, per * OB, per * KB * IB), bf16),
            V((group * layers, KB, blocks), i32),
            S((group * layers, KB, blocks), i32),
            V((2, group, rows, lanes), bf16),
            V((2, 8, lanes), f32),
            V((2 * classes, 8, lanes), f32),
            dma((2,)), dma((2,)),
            dma(()), dma((group,)), dma((group,)),
            dma(()), dma(()), dma(()),
            dma(()), dma((2,)),
            dma(()), dma(()),
            dma(()), dma((2,)), pltpu.SemaphoreType.REGULAR,
        ],
        compiler_params=pltpu.CompilerParams(collective_id=0, has_side_effects=True, vmem_limit_bytes=16 * 1024 * 1024),
    )(*operands)
    vmem_spec = pl.BlockSpec(memory_space=pltpu.VMEM)
    out, sums = pl.pallas_call(
        store,
        out_shape=(jax.ShapeDtypeStruct(out.shape, out.dtype), jax.ShapeDtypeStruct(sums.shape, sums.dtype)),
        in_specs=[vmem_spec] * 2,
        out_specs=(any_spec, any_spec),
        scratch_shapes=[dma((2,))],
    )(*(pltpu.with_memory_space_constraint(v, pltpu.VMEM) for v in (out, sums)))
    return out, sums.reshape(-1)


def solution(mesh):
    classes = mesh.shape["neu"] // KB
    in_specs = (P("neu", "img"), P("neu", "img"), P(None, "neu", None, None), P(None, "neu", None))
    out_specs = (P("neu", "img"), P(("img", "neu")))
    return jax.shard_map(
        functools.partial(on_device, classes, mesh.shape["img"] % 2 == 0), mesh=mesh, in_specs=in_specs,
        out_specs=out_specs, check_vma=False,
    )
```

time: 24.9 us -> 22.6 us (0.908)
  local copies, waits for them, and re-layouts: 1.22 us -> 0 us
  Pallas kernels: 22.8 us -> 21.8 us
    pallas_call x1, Pallas kernels: 22.8 us -> 21.1 us  [on_device(): pl.pallas_call(functools.partial(kernel, (classes, pairs, layers, rows, b...]
    unnamed x2 -> x0, local copies, waits for them, and re-layouts: 1.22 us -> none
    pallas_call x0 -> x1, Pallas kernels: none -> 0.72 us  [on_device(): pl.pallas_call(store, out_shape=(jax.ShapeDtypeStruct(out.shape, out.dtyp...]
where the time goes in v1:
time: 22.6 us; the launch traced here: 22.5 us
  Pallas kernels  21.8 us (96%)
  between operations  0.64 us (3%)
    pallas_call x1, Pallas kernels, on_device(): pl.pallas_call(functools.partial(kernel, (classes, pairs, layers, rows, b...  21.1 us
    pallas_call x1, Pallas kernels, on_device(): pl.pallas_call(store, out_shape=(jax.ShapeDtypeStruct(out.shape, out.dtyp...  0.72 us

profile of v1, /device:TPU:0, one launch (start us, length us, event | category | flops | bytes accessed | tf_op | source)
XLA Modules:
  0.0 22.5 jit_solution(659349611769343865)
XLA Ops:
  0.6 21.1 %shard_map.59 = (bf16[256,512]{1,0:T(8,128)(2,1)S(1)}, f32[1,32]{1,0:T(1,128)S(1)}) custom-call(bf16[256,512]{1,0:T(8,128)(2,1)} %val_hbm.1, s32[256,512]{1,0:T(8,128)} %mask_hbm.1, bf16[3,32,256]{2,1,0:T(8,128)(2,1)} %bitcast.5, s32[3,4,8]{2,1,0:T(4,128)} %bitcast.6), custom_call_target="tpu_custom_call" | custom-call | tf_op jit(solution)/shard_map/pallas_call | solution.py:285
  21.7 0.7 %shard_map.60 = (bf16[256,512]{1,0:T(8,128)(2,1)}, f32[1,32]{1,0:T(1,128)}) custom-call(bf16[256,512]{1,0:T(8,128)(2,1)S(1)} %get-tuple-element.6.out_ref, f32[1,32]{1,0:T(1,128)S(1)} %get-tuple-element.7.rs_ref), custom_call_target="tpu_custom_call" | custom-call | tf_op jit(solution)/shard_map/pallas_call | solution.py:320

commit v2 on v1

--- a/solution.py
+++ b/solution.py
@@ -30,7 +30,7 @@
 def kernel(
     geometry, val_hbm, mask_hbm, wt_hbm, idx_hbm, out_ref, rs_ref,
     val, mask, w_src, i_src, i_out, y0, xin, ya, yb, wt, wd, idx_v, idx_s, tiles, part, parts,
-    load_sem, own_sem, w_send, w_recv, f_recv, i_send, i_recv, s_sem, in_send, in_recv, o_send, o_recv,
+    load_sem, own_sem, w_send, w_recv, n_send, f_recv, i_send, i_recv, s_sem, in_send, in_recv, o_send, o_recv,
     r_send, r_recv, here_sem,
 ):
     classes, pairs, layers, rows, blocks, lanes = geometry
@@ -102,7 +102,10 @@
     def send_weights(l, z):
         n = q * layers + l
         remote(i_out.at[l], idx_v.at[n], i_send, i_recv, to(z, shift[l]))
-        remote(w_src.at[l, w_rows], wt.at[n, w_rows], w_send, w_recv.at[q], to(z, shift[l]))
+        if z is q:
+            remote(w_src.at[l], wt.at[n], n_send, w_recv.at[q], to(z, shift[l]))
+        else:
+            remote(w_src.at[l, w_rows], wt.at[n, w_rows], w_send, w_recv.at[q], to(z, shift[l]))
 
     def send_input(p, chunk, z):
         remote(y0.at[p], xin.at[chunk, q], in_send, in_recv.at[chunk], to(z, 0))
@@ -110,7 +113,7 @@
     unknown = [dc for dc in range(classes) if dc not in shift]
 
     def own_share(total):
-        row = jnp.sum(total, axis=0, keepdims=True)
+        row = total
         share = lanes // classes
         mine = jnp.zeros((1, share), jnp.float32)
         for j in range(classes):
@@ -127,11 +130,10 @@
             pl.semaphore_signal(here_sem, inc=1, device_id=to(near, dc), device_id_type=pl.DeviceIdType.MESH)
         wait(val, load_sem.at[0])
         wait(mask, load_sem.at[1])
+        wait(wt.at[pl.ds(0, 2 * layers), w_rows], w_send)
         for p in range(group):
             masked(p)
             send_input(p, p // 2, (far, near)[p % 2])
-        sent = wt.at[pl.ds(0, 2 * layers), w_rows]
-        wait(sent, w_send)
         wait(idx_v.at[pl.ds(0, 2 * layers)], i_send)
         wait(y0, in_send)
         wait(parts.at[pl.ds(0, classes)], r_recv.at[0])
@@ -151,6 +153,7 @@
                 idx_v[q * layers + l] = i_out[l]
         wait(val, load_sem.at[0])
         wait(mask, load_sem.at[1])
+        wait(wt.at[pl.ds(0, layers), w_rows], w_send)
         masked(0)
         send_input(0, 0, other)
         masked(1)
@@ -165,17 +168,18 @@
         n_of = lax.broadcasted_iota(jnp.int32, (width, width), 1) // OB
 
         def pieces_of(z):
-            first = local if z is q else 0
-            return wt.at[pl.ds(z * layers + first, layers - first), w_rows]
+            if z is q:
+                return wt.at[pl.ds(z * layers + local, layers - local)]
+            return wt.at[pl.ds(z * layers, layers), w_rows]
 
         def pass_on(z):
             here = pieces_of(z)
             wait(here, w_recv.at[z])
-            if pairs:
+            if pairs and z is not q:
                 remote(here, here, w_send, f_recv.at[z], twin)
 
         def prepare(z):
-            if pairs:
+            if pairs and z is not q:
                 wait(pieces_of(z), f_recv.at[z])
             for l in range(layers):
                 for g in range(blocks // per):
@@ -193,7 +197,7 @@
                 out.append(clamped.astype(jnp.bfloat16))
             return out
 
-        for z in (q, other, near, far):
+        for z,nm in ((q,'own'), (other,'oth'), (near,'nea'), (far,'far')):
             pass_on(z)
         wait(idx_v.at[pl.ds(0, group * layers - local)], i_recv)
         index_copy = pltpu.make_async_copy(idx_v, idx_s, s_sem)
@@ -222,7 +226,7 @@
 
             tile = near if chunk == 0 else q
             cols = pl.ds(pl.multiple_of(tile * lanes, lanes), lanes)
-            targets = (far, near, other, q)
+            targets = (near, far, other, q) if chunk else (near, far, other, q)
             total = jnp.zeros((8, lanes), jnp.float32)
 
             def send_tile(d):
@@ -238,7 +242,7 @@
                     if chunk == 0:
                         send_tile(d - 1)
                 ready = fresh
-            part[chunk] = total
+            part[chunk] = jnp.sum(total, axis=0, keepdims=True)
             for dc in range(chunk, classes):
                 where = to(q, dc) if chunk else to(near, dc)
                 remote(part.at[chunk], parts.at[chunk * classes + dc], r_send, r_recv.at[chunk], where)
@@ -249,9 +253,8 @@
         wait(parts.at[pl.ds(classes + 1, classes - 1)], r_recv.at[1])
         own_share(part[1] + sum(parts[classes + dc] for dc in range(1, classes)))
         if pairs:
-            wait(wt.at[pl.ds(0, 3 * layers - local)], w_send)
-        else:
-            wait(wt.at[pl.ds(0, 2 * layers - local)], w_send)
+            wait(wt.at[pl.ds(0, 3 * layers), w_rows], w_send)
+        wait(wt.at[pl.ds(0, layers - local)], n_send)
         wait(idx_v.at[pl.ds(0, 2 * layers - local)], i_send)
         wait(y0.at[pl.ds(0, 2)], in_send)
         wait(tiles, o_send)
@@ -305,10 +308,10 @@
             V((group * layers, KB, blocks), i32),
             S((group * layers, KB, blocks), i32),
             V((2, group, rows, lanes), bf16),
-            V((2, 8, lanes), f32),
-            V((2 * classes, 8, lanes), f32),
+            V((2, 1, lanes), f32),
+            V((2 * classes, 1, lanes), f32),
             dma((2,)), dma((2,)),
-            dma(()), dma((group,)), dma((group,)),
+            dma(()), dma((group,)), dma(()), dma((group,)),
             dma(()), dma(()), dma(()),
             dma(()), dma((2,)),
             dma(()), dma(()),

time: 22.6 us -> 21.2 us (0.938)
  Pallas kernels: 21.8 us -> 20.4 us
    pallas_call x1, Pallas kernels: 21.1 us -> 19.7 us  [on_device(): pl.pallas_call(functools.partial(kernel, (classes, pairs, layers, rows, b...]
where the time goes in v2:
time: 21.2 us; the launch traced here: 21 us
  Pallas kernels  20.4 us (96%)
  between operations  0.64 us (3%)
    pallas_call x1, Pallas kernels, on_device(): pl.pallas_call(functools.partial(kernel, (classes, pairs, layers, rows, b...  19.7 us
    pallas_call x1, Pallas kernels, on_device(): pl.pallas_call(store, out_shape=(jax.ShapeDtypeStruct(out.shape, out.dtyp...  0.72 us

profile of v2, /device:TPU:0, one launch (start us, length us, event | category | flops | bytes accessed | tf_op | source)
XLA Modules:
  0.0 21.0 jit_solution(5379603639483551145)
XLA Ops:
  0.6 19.7 %shard_map.59 = (bf16[256,512]{1,0:T(8,128)(2,1)S(1)}, f32[1,32]{1,0:T(1,128)S(1)}) custom-call(bf16[256,512]{1,0:T(8,128)(2,1)} %val_hbm.1, s32[256,512]{1,0:T(8,128)} %mask_hbm.1, bf16[3,32,256]{2,1,0:T(8,128)(2,1)} %bitcast.5, s32[3,4,8]{2,1,0:T(4,128)} %bitcast.6), custom_call_target="tpu_custom_call" | custom-call | tf_op jit(solution)/shard_map/pallas_call | solution.py:288
  20.3 0.7 %shard_map.60 = (bf16[256,512]{1,0:T(8,128)(2,1)}, f32[1,32]{1,0:T(1,128)}) custom-call(bf16[256,512]{1,0:T(8,128)(2,1)S(1)} %get-tuple-element.6.out_ref, f32[1,32]{1,0:T(1,128)S(1)} %get-tuple-element.7.rs_ref), custom_call_target="tpu_custom_call" | custom-call | tf_op jit(solution)/shard_map/pallas_call | solution.py:323

commit v3 on v2

--- a/solution.py
+++ b/solution.py
@@ -178,8 +178,8 @@
             if pairs and z is not q:
                 remote(here, here, w_send, f_recv.at[z], twin)
 
-        def prepare(z):
-            if pairs and z is not q:
+        def prepare(z, take=True):
+            if pairs and z is not q and take:
                 wait(pieces_of(z), f_recv.at[z])
             for l in range(layers):
                 for g in range(blocks // per):
@@ -197,7 +197,7 @@
                 out.append(clamped.astype(jnp.bfloat16))
             return out
 
-        for z,nm in ((q,'own'), (other,'oth'), (near,'nea'), (far,'far')):
+        for z in (other, near, far, q):
             pass_on(z)
         wait(idx_v.at[pl.ds(0, group * layers - local)], i_recv)
         index_copy = pltpu.make_async_copy(idx_v, idx_s, s_sem)
@@ -205,14 +205,17 @@
         prepare(q)
         prepare(other)
         prepare(near)
-        prepare(far)
         index_copy.wait()
+        if pairs:
+            wait(pieces_of(far), f_recv.at[far])
         pl.semaphore_wait(here_sem, len(unknown))
 
         for chunk in range(2):
             own_rows = y0[2 + chunk].astype(jnp.float32)
             ya[pl.ds(q * run_blocks, run_blocks)] = own_rows.reshape(run_blocks, IB, lanes)
             wait(xin.at[chunk, pl.ds(0, group - 1)], in_recv.at[chunk])
+            if chunk == 0:
+                prepare(far, False)
             for z in (other, near, far):
                 ya[pl.ds(z * run_blocks, run_blocks)] = xin[chunk, z].astype(jnp.float32).reshape(run_blocks, IB, lanes)
 
@@ -226,7 +229,7 @@
 
             tile = near if chunk == 0 else q
             cols = pl.ds(pl.multiple_of(tile * lanes, lanes), lanes)
-            targets = (near, far, other, q) if chunk else (near, far, other, q)
+            targets = (near, far, other, q)
             total = jnp.zeros((8, lanes), jnp.float32)
 
             def send_tile(d):
@@ -264,9 +267,12 @@
 
 def store(out_ref, rs_ref, out_hbm, rs_hbm, sems):
     a = pltpu.make_async_copy(out_ref, out_hbm, sems.at[0])
+    step = out_ref.shape[0] // 4
     b = pltpu.make_async_copy(rs_ref, rs_hbm, sems.at[1])
-    a.start()
     b.start()
+    for n in range(4):
+        rows = pl.ds(n * step, step)
+        pltpu.make_async_copy(out_ref.at[rows], out_hbm.at[rows], sems.at[0]).start()
     a.wait()
     b.wait()
 

time: 21.2 us -> 21.1 us (level)
  no operation moved by 1% of the time
where the time goes in v3:
time: 21.1 us; the launch traced here: 20.9 us
  Pallas kernels  20.2 us (96%)
  between operations  0.64 us (3%)
    pallas_call x1, Pallas kernels, on_device(): pl.pallas_call(functools.partial(kernel, (classes, pairs, layers, rows, b...  19.5 us
    pallas_call x1, Pallas kernels, on_device(): pl.pallas_call(store, out_shape=(jax.ShapeDtypeStruct(out.shape, out.dtyp...  0.72 us

profile of v3, /device:TPU:0, one launch (start us, length us, event | category | flops | bytes accessed | tf_op | source)
XLA Modules:
  0.0 20.9 jit_solution(16623140762495162302)
XLA Ops:
  0.6 19.5 %shard_map.59 = (bf16[256,512]{1,0:T(8,128)(2,1)S(1)}, f32[1,32]{1,0:T(1,128)S(1)}) custom-call(bf16[256,512]{1,0:T(8,128)(2,1)} %val_hbm.1, s32[256,512]{1,0:T(8,128)} %mask_hbm.1, bf16[3,32,256]{2,1,0:T(8,128)(2,1)} %bitcast.5, s32[3,4,8]{2,1,0:T(4,128)} %bitcast.6), custom_call_target="tpu_custom_call" | custom-call | tf_op jit(solution)/shard_map/pallas_call | solution.py:294
  20.2 0.7 %shard_map.60 = (bf16[256,512]{1,0:T(8,128)(2,1)}, f32[1,32]{1,0:T(1,128)}) custom-call(bf16[256,512]{1,0:T(8,128)(2,1)S(1)} %get-tuple-element.6.out_ref, f32[1,32]{1,0:T(1,128)S(1)} %get-tuple-element.7.rs_ref), custom_call_target="tpu_custom_call" | custom-call | tf_op jit(solution)/shard_map/pallas_call | solution.py:329

commit v4 on v3

--- a/solution.py
+++ b/solution.py
@@ -101,11 +101,13 @@
 
     def send_weights(l, z):
         n = q * layers + l
-        remote(i_out.at[l], idx_v.at[n], i_send, i_recv, to(z, shift[l]))
         if z is q:
             remote(w_src.at[l], wt.at[n], n_send, w_recv.at[q], to(z, shift[l]))
         else:
             remote(w_src.at[l, w_rows], wt.at[n, w_rows], w_send, w_recv.at[q], to(z, shift[l]))
+
+    def send_indices(l, z):
+        remote(i_out.at[l], idx_v.at[q * layers + l], i_send, i_recv, to(z, shift[l]))
 
     def send_input(p, chunk, z):
         remote(y0.at[p], xin.at[chunk, q], in_send, in_recv.at[chunk], to(z, 0))
@@ -126,6 +128,9 @@
         for z in (far, near):
             for l in range(layers):
                 send_weights(l, z)
+        for z in (far, near):
+            for l in range(layers):
+                send_indices(l, z)
         for dc in unknown:
             pl.semaphore_signal(here_sem, inc=1, device_id=to(near, dc), device_id_type=pl.DeviceIdType.MESH)
         wait(val, load_sem.at[0])
@@ -151,13 +156,16 @@
             else:
                 wt[q * layers + l] = w_src[l]
                 idx_v[q * layers + l] = i_out[l]
+        for l in range(layers):
+            send_indices(l, other)
+            if shift[l]:
+                send_indices(l, q)
         wait(val, load_sem.at[0])
         wait(mask, load_sem.at[1])
         wait(wt.at[pl.ds(0, layers), w_rows], w_send)
         masked(0)
         send_input(0, 0, other)
         masked(1)
-        send_input(1, 1, other)
         masked(2)
         masked(3)
 
@@ -197,8 +205,11 @@
                 out.append(clamped.astype(jnp.bfloat16))
             return out
 
-        for z in (other, near, far, q):
-            pass_on(z)
+        pass_on(other)
+        pass_on(near)
+        send_input(1, 1, other)
+        pass_on(far)
+        pass_on(q)
         wait(idx_v.at[pl.ds(0, group * layers - local)], i_recv)
         index_copy = pltpu.make_async_copy(idx_v, idx_s, s_sem)
         index_copy.start()

time: 21.1 us -> 21 us (level)
  no operation moved by 1% of the time
where the time goes in v4:
time: 21 us; the launch traced here: 20.9 us
  Pallas kernels  20.2 us (96%)
  between operations  0.64 us (3%)
    pallas_call x1, Pallas kernels, on_device(): pl.pallas_call(functools.partial(kernel, (classes, pairs, layers, rows, b...  19.5 us
    pallas_call x1, Pallas kernels, on_device(): pl.pallas_call(store, out_shape=(jax.ShapeDtypeStruct(out.shape, out.dtyp...  0.72 us

profile of v4, /device:TPU:0, one launch (start us, length us, event | category | flops | bytes accessed | tf_op | source)
XLA Modules:
  0.0 20.9 jit_solution(11598895857452114001)
XLA Ops:
  0.6 19.5 %shard_map.59 = (bf16[256,512]{1,0:T(8,128)(2,1)S(1)}, f32[1,32]{1,0:T(1,128)S(1)}) custom-call(bf16[256,512]{1,0:T(8,128)(2,1)} %val_hbm.1, s32[256,512]{1,0:T(8,128)} %mask_hbm.1, bf16[3,32,256]{2,1,0:T(8,128)(2,1)} %bitcast.5, s32[3,4,8]{2,1,0:T(4,128)} %bitcast.6), custom_call_target="tpu_custom_call" | custom-call | tf_op jit(solution)/shard_map/pallas_call | solution.py:305
  20.1 0.7 %shard_map.60 = (bf16[256,512]{1,0:T(8,128)(2,1)}, f32[1,32]{1,0:T(1,128)}) custom-call(bf16[256,512]{1,0:T(8,128)(2,1)S(1)} %get-tuple-element.6.out_ref, f32[1,32]{1,0:T(1,128)S(1)} %get-tuple-element.7.rs_ref), custom_call_target="tpu_custom_call" | custom-call | tf_op jit(solution)/shard_map/pallas_call | solution.py:340
